TPU v7x, 32 devices: a whole 2x2x4 slice. The times are simulated.
32 devices in a mesh: blk: 8 (over z, x), lane: 4 (over y, core).
Axes of the slice: x: 2, y: 2, z: 4, core: 2. Of those that a mesh axis runs over, the one named last changes fastest.
Arguments:
- left_factor: bfloat16 [4096, 512], P('blk'), may hold values from -6 to 6
- right_factor: bfloat16 [4, 4096, 512], P('lane', 'blk'), may hold values from -6 to 6
- observed: bfloat16 [4, 4, 512, 4096], P('lane', None, None, 'blk'), may hold values from -6 to 6
- row_codes: int32 [4096], P('blk'), may hold values from 0 to 1073741823
- shift_codes: int32 [4, 4, 4096], P('lane', None, 'blk'), may hold values from 0 to 29
Outputs:
- left_out: bfloat16 [4096, 512], P('blk')
- right_out: bfloat16 [4, 4096, 512], P('lane', 'blk')
Inputs may be any that keep to these rules, and one draw needn't show every extreme that they name: `row_codes`: each row's word carries thirty independent sampling bits. `shift_codes`: A bit number for each lane, cycle step and visited tile entry column.
All inputs are finite; a program needn't handle non-finite values.
Results may differ from a plain program's by a relative error of at most 0.013.
Values may be sent and summed in bfloat16 or wider, within the bound.
A program may use at most 64 MiB of HBM per device.

v0:
```python
import math
import jax
import jax.numpy as jnp
from jax import lax
from jax.sharding import PartitionSpec as P

step_right = 0.25
step_left = 0.1


def passed_along(value, axis, steps):
    count = lax.axis_size(axis)
    pairs = [(source, (source + steps) % count) for source in range(count)]
    return lax.ppermute(value, axis, pairs)


def visit_tile(right_part, left_factor, target, row_codes, shifts, root_scale):
    predicted = (
        lax.dot_general(
            right_part, left_factor, (((1,), (1,)), ((), ())), preferred_element_type=jnp.float32
        )
        * root_scale
    )
    sample_bits = jnp.right_shift(row_codes[None, :], shifts[:, None]) & 1
    error_tile = jnp.where(sample_bits == 1, predicted - target.astype(jnp.float32), 0.0).astype(
        jnp.bfloat16
    )
    grad_right = jnp.dot(error_tile, left_factor, preferred_element_type=jnp.float32)
    grad_left = lax.dot_general(
        error_tile, right_part, (((0,), (0,)), ((), ())), preferred_element_type=jnp.float32
    )
    updated = (right_part.astype(jnp.float32) - step_right * root_scale * grad_right).astype(
        jnp.bfloat16
    )
    return (updated, grad_left)


def local(left_factor, right_factor, observed, row_codes, shift_codes):
    rank_size = left_factor.shape[1]
    root_scale = 1.0 / math.sqrt(rank_size)
    cycle_steps = observed.shape[1]
    column_count = observed.shape[2]
    right_now = right_factor[0]
    grad_sum = jnp.zeros(left_factor.shape, jnp.float32)
    for cycle_step in range(cycle_steps):
        target = observed[0, cycle_step]
        shifts = shift_codes[0, cycle_step]
        last_step = cycle_step + 1 == cycle_steps
        half_cols = column_count // 2
        pieces = []
        for portion in range(2):
            first_col = portion * half_cols
            updated, grad_left = visit_tile(
                right_now[first_col : first_col + half_cols],
                left_factor,
                target[first_col : first_col + half_cols],
                row_codes,
                shifts[first_col : first_col + half_cols],
                root_scale,
            )
            grad_sum = grad_sum + grad_left
            pieces.append(updated if last_step else passed_along(updated, "blk", 1))
        right_now = jnp.concatenate(pieces, axis=0)
    summed = lax.psum(grad_sum.astype(jnp.bfloat16), "lane").astype(jnp.float32)
    left_out = (left_factor.astype(jnp.float32) - step_left * root_scale * summed).astype(
        jnp.bfloat16
    )
    return (left_out, right_now[None])


def solution(mesh):
    in_specs = (
        P("blk", None),
        P("lane", "blk", None),
        P("lane", None, None, "blk"),
        P("blk"),
        P("lane", None, "blk"),
    )
    out_specs = (P("blk", None), P("lane", "blk", None))
    return jax.shard_map(local, mesh=mesh, in_specs=in_specs, out_specs=out_specs, check_vma=False)
```

profile of v0, /device:TPU:0, one launch (start us, length us, event | category | flops | bytes accessed | tf_op | source)
XLA Modules:
  0.0 94.1 jit_solution(8575521751137089536)
XLA Ops:
  7.2 0.0 copy-start
  7.2 0.0 copy-start.3
  7.2 0.0 copy-start.1
  7.2 0.0 all-reduce.2.cloned.1.call-start
  7.2 0.0 copy-start.2
  7.3 0.9 fusion.43
  8.2 1.6 %fusion.27 = bf16[256,512]{1,0:T(8,128)(2,1)S(1)} fusion(bf16[512,512]{1,0:T(8,128)(2,1)} %param.5, bf16[1,4,512,512]{3,2,1,0:T(8,128)(2,1)} %param.7, s32[256]{0:T(256)S(1)} %bitcast.97, s32[512]{0:T(512)} %param.8, bf16[1,512,512]{2,1,0:T(8,128)(2,1)} %param.6), kind=kOutput, calls=%fused_computation.45 | convolution fusion | flops 135266304 | bytes 1313792 | tf_op jit(solution)/shard_map/dot_general | solution.py:19
  9.8 0.0 copy-done
  9.8 0.3 fusion.25
  10.1 3.0 %collective-permute-start.1 = (bf16[256,512]{1,0:T(8,128)(2,1)S(1)}, bf16[256,512]{1,0:T(8,128)(2,1)S(1)}, u32[]{:S(2)}, u32[]{:S(2)}) collective-permute-start(bf16[256,512]{1,0:T(8,128)(2,1)S(1)} %fusion.25), channel_id=1, source_target_pairs={{0,4},{4,8},{8,12},{12,16},{16,20},{20,24},{24,28},{28,0},{1,5},{5... | collective-permute-start | bytes 786440 | tf_op jit(solution)/shard_map/ppermute | solution.py:14
  13.1 0.0 copy-done.3
  13.1 0.4 fusion.26
  13.5 0.3 fusion.24
  13.8 1.6 %collective-permute-start = (bf16[256,512]{1,0:T(8,128)(2,1)S(1)}, bf16[256,512]{1,0:T(8,128)(2,1)S(1)}, u32[]{:S(2)}, u32[]{:S(2)}) collective-permute-start(bf16[256,512]{1,0:T(8,128)(2,1)S(1)} %fusion.24), channel_id=1, source_target_pairs={{0,4},{4,8},{8,12},{12,16},{16,20},{20,24},{24,28},{28,0},{1,5},{5... | collective-permute-start | bytes 786440 | tf_op jit(solution)/shard_map/ppermute | solution.py:14
  15.4 0.3 fusion.36
  15.7 0.3 convolution_add_fusion.1
  16.1 7.2 %collective-permute-done.1 = bf16[256,512]{1,0:T(8,128)(2,1)S(1)} collective-permute-done((bf16[256,512]{1,0:T(8,128)(2,1)S(1)}, bf16[256,512]{1,0:T(8,128)(2,1)S(1)}, u32[]{:S(2)}, u32[]{:S(2)}) %collective-permute-start.1) | collective-permute-done | bytes 262176 | tf_op jit(solution)/shard_map/ppermute | solution.py:14
  23.3 0.4 fusion.29
  23.7 0.3 subtract_convert_fusion.5
  24.0 0.1 collective-permute-start.3
  24.1 4.3 %collective-permute-done = bf16[256,512]{1,0:T(8,128)(2,1)S(1)} collective-permute-done((bf16[256,512]{1,0:T(8,128)(2,1)S(1)}, bf16[256,512]{1,0:T(8,128)(2,1)S(1)}, u32[]{:S(2)}, u32[]{:S(2)}) %collective-permute-start) | collective-permute-done | bytes 262176 | tf_op jit(solution)/shard_map/ppermute | solution.py:14
  28.4 0.4 fusion.28
  28.8 0.3 subtract_convert_fusion.6
  29.1 0.1 collective-permute-start.2
  29.1 0.3 fusion.44
  29.5 4.5 %collective-permute-done.3 = bf16[256,512]{1,0:T(8,128)(2,1)S(1)} collective-permute-done((bf16[256,512]{1,0:T(8,128)(2,1)S(1)}, bf16[256,512]{1,0:T(8,128)(2,1)S(1)}, u32[]{:S(2)}, u32[]{:S(2)}) %collective-permute-start.3) | collective-permute-done | bytes 262176 | tf_op jit(solution)/shard_map/ppermute | solution.py:14
  34.0 0.4 fusion.31
  34.4 0.3 subtract_convert_fusion.3
  34.7 0.1 collective-permute-start.5
  34.8 6.2 %collective-permute-done.2 = bf16[256,512]{1,0:T(8,128)(2,1)S(1)} collective-permute-done((bf16[256,512]{1,0:T(8,128)(2,1)S(1)}, bf16[256,512]{1,0:T(8,128)(2,1)S(1)}, u32[]{:S(2)}, u32[]{:S(2)}) %collective-permute-start.2) | collective-permute-done | bytes 262176 | tf_op jit(solution)/shard_map/ppermute | solution.py:14
  41.0 0.4 fusion.30
  41.4 0.3 subtract_convert_fusion.4
  41.7 0.1 collective-permute-start.4
  41.8 0.3 fusion.45
  42.1 0.3 fusion.46
  42.4 8.4 %collective-permute-done.4 = bf16[256,512]{1,0:T(8,128)(2,1)S(1)} collective-permute-done((bf16[256,512]{1,0:T(8,128)(2,1)S(1)}, bf16[256,512]{1,0:T(8,128)(2,1)S(1)}, u32[]{:S(2)}, u32[]{:S(2)}) %collective-permute-start.4) | collective-permute-done | bytes 262176 | tf_op jit(solution)/shard_map/ppermute | solution.py:14
  50.8 0.4 fusion.32
  51.2 0.3 fusion.47
  51.5 0.0 collective-permute-done.5
  51.5 0.4 fusion.33
  51.9 0.3 fusion.48
  52.2 1.3 %fusion.5 = bf16[512,512]{1,0:T(8,128)(2,1)} fusion(f32[512,512]{1,0:T(8,128)S(1)} %fusion.48, f32[512,512]{1,0:T(8,128)S(1)} %fusion.47, f32[512,512]{1,0:T(8,128)S(1)} %fusion.46, f32[512,512]{1,0:T(8,128)S(1)} %fusion.45, f32[512,512]{1,0:T(8,128)S(1)} %fusion.44, f32[512,512]{1,0:T(8,128)S(1)} %convolution_add_fusion.1, ...), kind=kOutput, calls=%fused_computation.7 | convolution fusion | flops 136052736 | bytes 7340032 | tf_op jit(solution)/shard_map/dot_general | solution.py:29
  53.5 0.0 all-reduce.2.cloned.1.call-update
  53.5 0.3 subtract_convert_fusion.1
  53.9 0.3 subtract_convert_fusion.2
  54.2 0.8 maximum_bitcast_fusion
  55.0 30.3 %all-reduce.2.cloned.1.call-done = bf16[512,512]{1,0:T(8,128)(2,1)} async-done(((bf16[512,512]{1,0:T(8,128)(2,1)}), bf16[512,512]{1,0:T(8,128)(2,1)}) %all-reduce.2.cloned.1.call-update) | async-done | bytes 524304 | tf_op jit(solution)/shard_map/psum | solution.py:64
  85.3 2.0 %subtract_convert_fusion = bf16[512,512]{1,0:T(8,128)(2,1)} fusion(bf16[512,512]{1,0:T(8,128)(2,1)} %all-reduce.2.cloned.1.call-done, bf16[512,512]{1,0:T(8,128)(2,1)S(1)} %copy-done), kind=kLoop, calls=%fused_computation.52 | loop fusion | flops 1310720 | bytes 1572864 | tf_op jit(solution)/shard_map/convert_element_type | solution.py:65
  (2 shorter events, 0.0 us)
Async XLA Ops:
  7.2 2.6 %copy-start = (bf16[512,512]{1,0:T(8,128)(2,1)S(1)}, bf16[512,512]{1,0:T(8,128)(2,1)}, u32[]{:S(2)}) copy-start(bf16[512,512]{1,0:T(8,128)(2,1)} %param.5) | copy-start | bytes 1572868
  7.2 5.9 %copy-start.3 = (s32[512]{0:T(512)S(1)}, s32[512]{0:T(512)}, u32[]{:S(2)}) copy-start(s32[512]{0:T(512)} %param.8) | copy-start | bytes 6148
  7.2 2.6 %copy-start.1 = (bf16[1,512,512]{2,1,0:T(8,128)(2,1)S(1)}, bf16[1,512,512]{2,1,0:T(8,128)(2,1)}, u32[]{:S(2)}) copy-start(bf16[1,512,512]{2,1,0:T(8,128)(2,1)} %param.6) | copy-start | bytes 1572868
  7.2 78.1 %all-reduce.2.cloned.1.call-start = ((), (), s32[]{:S(2)}) async-start(), calls=%async_computation | async-start | bytes 1048576 | tf_op jit(solution)/shard_map/psum | solution.py:64
  7.2 5.9 %copy-start.2 = (bf16[1,4,512,512]{3,2,1,0:T(8,128)(2,1)S(1)}, bf16[1,4,512,512]{3,2,1,0:T(8,128)(2,1)}, u32[]{:S(2)}) copy-start(bf16[1,4,512,512]{3,2,1,0:T(8,128)(2,1)} %param.7) | copy-start | bytes 6291460
  10.1 13.2 %collective-permute-start.1 = (bf16[256,512]{1,0:T(8,128)(2,1)S(1)}, bf16[256,512]{1,0:T(8,128)(2,1)S(1)}, u32[]{:S(2)}, u32[]{:S(2)}) collective-permute-start(bf16[256,512]{1,0:T(8,128)(2,1)S(1)} %fusion.25), channel_id=1, source_target_pairs={{0,4},{4,8},{8,12},{12,16},{16,20},{20,24},{24,28},{28,0},{1,5},{5... | collective-permute-start | bytes 786440 | tf_op jit(solution)/shard_map/ppermute | solution.py:14
  13.8 14.6 %collective-permute-start = (bf16[256,512]{1,0:T(8,128)(2,1)S(1)}, bf16[256,512]{1,0:T(8,128)(2,1)S(1)}, u32[]{:S(2)}, u32[]{:S(2)}) collective-permute-start(bf16[256,512]{1,0:T(8,128)(2,1)S(1)} %fusion.24), channel_id=1, source_target_pairs={{0,4},{4,8},{8,12},{12,16},{16,20},{20,24},{24,28},{28,0},{1,5},{5... | collective-permute-start | bytes 786440 | tf_op jit(solution)/shard_map/ppermute | solution.py:14
  24.0 10.0 %collective-permute-start.3 = (bf16[256,512]{1,0:T(8,128)(2,1)S(1)}, bf16[256,512]{1,0:T(8,128)(2,1)S(1)}, u32[]{:S(2)}, u32[]{:S(2)}) collective-permute-start(bf16[256,512]{1,0:T(8,128)(2,1)S(1)} %subtract_convert_fusion.5), channel_id=1, source_target_pairs={{0,4},{4,8},{8,12},{12,16},{16,20},{20,24},{24,28},{28,0},{1,5},{5... | collective-permute-start | bytes 786440 | tf_op jit(solution)/shard_map/ppermute | solution.py:14
  29.1 11.9 %collective-permute-start.2 = (bf16[256,512]{1,0:T(8,128)(2,1)S(1)}, bf16[256,512]{1,0:T(8,128)(2,1)S(1)}, u32[]{:S(2)}, u32[]{:S(2)}) collective-permute-start(bf16[256,512]{1,0:T(8,128)(2,1)S(1)} %subtract_convert_fusion.6), channel_id=1, source_target_pairs={{0,4},{4,8},{8,12},{12,16},{16,20},{20,24},{24,28},{28,0},{1,5},{5... | collective-permute-start | bytes 786440 | tf_op jit(solution)/shard_map/ppermute | solution.py:14
  34.7 16.8 %collective-permute-start.5 = (bf16[256,512]{1,0:T(8,128)(2,1)S(1)}, bf16[256,512]{1,0:T(8,128)(2,1)S(1)}, u32[]{:S(2)}, u32[]{:S(2)}) collective-permute-start(bf16[256,512]{1,0:T(8,128)(2,1)S(1)} %subtract_convert_fusion.3), channel_id=1, source_target_pairs={{0,4},{4,8},{8,12},{12,16},{16,20},{20,24},{24,28},{28,0},{1,5},{5... | collective-permute-start | bytes 786440 | tf_op jit(solution)/shard_map/ppermute | solution.py:14
  41.7 9.1 %collective-permute-start.4 = (bf16[256,512]{1,0:T(8,128)(2,1)S(1)}, bf16[256,512]{1,0:T(8,128)(2,1)S(1)}, u32[]{:S(2)}, u32[]{:S(2)}) collective-permute-start(bf16[256,512]{1,0:T(8,128)(2,1)S(1)} %subtract_convert_fusion.4), channel_id=1, source_target_pairs={{0,4},{4,8},{8,12},{12,16},{16,20},{20,24},{24,28},{28,0},{1,5},{5... | collective-permute-start | bytes 786440 | tf_op jit(solution)/shard_map/ppermute | solution.py:14
Sparse Core Ops, SparseCore 0:
  53.7 31.5 all-reduce.1
where the time goes:
time: 94.3 us; the launch traced here: 94.1 us
  waiting for transfers between devices  61.1 us (65%)
  between operations  14.3 us (15%)
  matrix products  10.2 us (11%)
  starting transfers between devices  4.89 us (5%)
  other arithmetic  2.82 us (3%)
  local copies, waits for them, and re-layouts  0.95 us (1%)
    ppermute x6, waiting for transfers between devices, passed_along(): return lax.ppermute(value, axis, pairs)  30.7 us
    psum x1, waiting for transfers between devices, local(): summed = lax.psum(grad_sum.astype(jnp.bfloat16), 'lane').astype(jnp.float32)  30.3 us
    ppermute x6, starting transfers between devices, passed_along(): return lax.ppermute(value, axis, pairs)  4.85 us
    dot_general x8, matrix products, visit_tile(): lax.dot_general(right_part, left_factor, (((1,), (1,)), ((), ())), prefer...  4.16 us
    dot_general x8, matrix products, visit_tile(): lax.dot_general(error_tile, right_part, (((0,), (0,)), ((), ())), preferr...  3.58 us
    dot_general x8, matrix products, visit_tile(): jnp.dot(error_tile, left_factor, preferred_element_type=jnp.float32)  2.42 us
    convert_element_type x1, other arithmetic, local(): (left_factor.astype(jnp.float32) - step_left * root_scale * summed).astyp...  1.99 us
  transfers between devices with their start and end apart: 7, of which 6 were waited for; matrix products, arithmetic and copies ran while one was open for 8% of the time, Pallas kernels for 0%

commit v1 on v0

--- a/solution.py
+++ b/solution.py
@@ -61,7 +61,9 @@
             grad_sum = grad_sum + grad_left
             pieces.append(updated if last_step else passed_along(updated, "blk", 1))
         right_now = jnp.concatenate(pieces, axis=0)
-    summed = lax.psum(grad_sum.astype(jnp.bfloat16), "lane").astype(jnp.float32)
+    summed = jnp.sum(lax.all_gather(grad_sum.astype(jnp.bfloat16), axis_name="lane"), 0).astype(
+        jnp.float32
+    )
     left_out = (left_factor.astype(jnp.float32) - step_left * root_scale * summed).astype(
         jnp.bfloat16
     )

time: 94.3 us -> 85.6 us (0.908)
  waiting for transfers between devices: 61.1 us -> 50.2 us
  other arithmetic: 2.82 us -> 3.96 us
    psum x1 -> x0, waiting for transfers between devices: 30.3 us -> none  [local(): summed = lax.psum(grad_sum.astype(jnp.bfloat16), 'lane').astype(jnp.float32)]
    all_gather x0 -> x1, waiting for transfers between devices: none -> 19.5 us  [local(): lax.all_gather(grad_sum.astype(jnp.bfloat16), axis_name='lane')]
    reduce_sum x0 -> x1, other arithmetic: none -> 2.18 us  [local(): jnp.sum(lax.all_gather(grad_sum.astype(jnp.bfloat16), axis_name='lane'), 0)]
    convert_element_type x1, other arithmetic: 1.99 us -> 0.95 us  [local(): (left_factor.astype(jnp.float32) - step_left * root_scale * summed).astyp...]
where the time goes in v1:
time: 85.6 us; the launch traced here: 85.4 us
  waiting for transfers between devices  50.2 us (59%)
  between operations  14.3 us (17%)
  matrix products  11.1 us (13%)
  starting transfers between devices  4.89 us (6%)
  other arithmetic  3.96 us (5%)
  local copies, waits for them, and re-layouts  0.95 us (1%)
    ppermute x6, waiting for transfers between devices, passed_along(): return lax.ppermute(value, axis, pairs)  30.8 us
    all_gather x1, waiting for transfers between devices, local(): lax.all_gather(grad_sum.astype(jnp.bfloat16), axis_name='lane')  19.5 us
    dot_general x8, matrix products, visit_tile(): lax.dot_general(right_part, left_factor, (((1,), (1,)), ((), ())), prefer...  5.08 us
    ppermute x6, starting transfers between devices, passed_along(): return lax.ppermute(value, axis, pairs)  4.85 us
    dot_general x8, matrix products, visit_tile(): lax.dot_general(error_tile, right_part, (((0,), (0,)), ((), ())), preferr...  3.58 us
    dot_general x8, matrix products, visit_tile(): jnp.dot(error_tile, left_factor, preferred_element_type=jnp.float32)  2.44 us
    reduce_sum x1, other arithmetic, local(): jnp.sum(lax.all_gather(grad_sum.astype(jnp.bfloat16), axis_name='lane'), 0)  2.18 us
  transfers between devices with their start and end apart: 7, of which 6 were waited for; matrix products, arithmetic and copies ran while one was open for 8% of the time, Pallas kernels for 0%

profile of v1, /device:TPU:0, one launch (start us, length us, event | category | flops | bytes accessed | tf_op | source)
XLA Modules:
  0.0 85.4 jit_solution(14675379530674145588)
XLA Ops:
  7.2 0.0 copy-start
  7.2 0.0 copy-start.3
  7.2 0.0 copy-start.1
  7.2 0.0 copy-start.2
  7.2 0.0 all-gather.3.cloned.1.call-start
  7.3 0.9 %fusion.43 = (s32[1,1,256]{2,1,0:T(1,128)S(1)}, s32[1,1,256]{2,1,0:T(1,128)S(1)}, s32[1,1,256]{2,1,0:T(1,128)S(1)}, s32[1,1,256]{2,1,0:T(1,128)S(1)}, s32[1,1,25...) fusion(s32[1,4,512]{2,1,0:T(4,128)} %param.9), kind=kLoop, calls=%fused_computation.77 | loop fusion | bytes 16384 | tf_op jit(solution)/shard_map/slice | solution.py:58
  8.2 1.6 %fusion.27 = bf16[256,512]{1,0:T(8,128)(2,1)S(1)} fusion(bf16[512,512]{1,0:T(8,128)(2,1)} %param.5, bf16[1,4,512,512]{3,2,1,0:T(8,128)(2,1)} %param.7, s32[256]{0:T(256)S(1)} %bitcast.99, s32[512]{0:T(512)} %param.8, bf16[1,512,512]{2,1,0:T(8,128)(2,1)} %param.6), kind=kOutput, calls=%fused_computation.45 | convolution fusion | flops 135266304 | bytes 1313792 | tf_op jit(solution)/shard_map/dot_general | solution.py:19
  9.8 0.0 copy-done
  9.8 0.3 fusion.25
  10.1 3.0 %collective-permute-start.1 = (bf16[256,512]{1,0:T(8,128)(2,1)S(1)}, bf16[256,512]{1,0:T(8,128)(2,1)S(1)}, u32[]{:S(2)}, u32[]{:S(2)}) collective-permute-start(bf16[256,512]{1,0:T(8,128)(2,1)S(1)} %fusion.25), channel_id=1, source_target_pairs={{0,4},{4,8},{8,12},{12,16},{16,20},{20,24},{24,28},{28,0},{1,5},{5... | collective-permute-start | bytes 786440 | tf_op jit(solution)/shard_map/ppermute | solution.py:14
  13.1 0.4 fusion.26
  13.5 0.3 fusion.24
  13.8 1.6 %collective-permute-start = (bf16[256,512]{1,0:T(8,128)(2,1)S(1)}, bf16[256,512]{1,0:T(8,128)(2,1)S(1)}, u32[]{:S(2)}, u32[]{:S(2)}) collective-permute-start(bf16[256,512]{1,0:T(8,128)(2,1)S(1)} %fusion.24), channel_id=1, source_target_pairs={{0,4},{4,8},{8,12},{12,16},{16,20},{20,24},{24,28},{28,0},{1,5},{5... | collective-permute-start | bytes 786440 | tf_op jit(solution)/shard_map/ppermute | solution.py:14
  15.4 0.3 fusion.36
  15.7 0.3 convolution_add_fusion.1
  16.1 7.2 %collective-permute-done.1 = bf16[256,512]{1,0:T(8,128)(2,1)S(1)} collective-permute-done((bf16[256,512]{1,0:T(8,128)(2,1)S(1)}, bf16[256,512]{1,0:T(8,128)(2,1)S(1)}, u32[]{:S(2)}, u32[]{:S(2)}) %collective-permute-start.1) | collective-permute-done | bytes 262176 | tf_op jit(solution)/shard_map/ppermute | solution.py:14
  23.3 0.4 fusion.29
  23.7 0.3 subtract_convert_fusion.5
  24.0 0.1 collective-permute-start.3
  24.1 4.3 %collective-permute-done = bf16[256,512]{1,0:T(8,128)(2,1)S(1)} collective-permute-done((bf16[256,512]{1,0:T(8,128)(2,1)S(1)}, bf16[256,512]{1,0:T(8,128)(2,1)S(1)}, u32[]{:S(2)}, u32[]{:S(2)}) %collective-permute-start) | collective-permute-done | bytes 262176 | tf_op jit(solution)/shard_map/ppermute | solution.py:14
  28.4 0.4 fusion.28
  28.8 0.3 subtract_convert_fusion.6
  29.1 0.1 collective-permute-start.2
  29.1 0.3 fusion.44
  29.5 4.5 %collective-permute-done.3 = bf16[256,512]{1,0:T(8,128)(2,1)S(1)} collective-permute-done((bf16[256,512]{1,0:T(8,128)(2,1)S(1)}, bf16[256,512]{1,0:T(8,128)(2,1)S(1)}, u32[]{:S(2)}, u32[]{:S(2)}) %collective-permute-start.3) | collective-permute-done | bytes 262176 | tf_op jit(solution)/shard_map/ppermute | solution.py:14
  34.0 0.4 fusion.31
  34.4 0.3 subtract_convert_fusion.3
  34.7 0.1 collective-permute-start.5
  34.8 6.2 %collective-permute-done.2 = bf16[256,512]{1,0:T(8,128)(2,1)S(1)} collective-permute-done((bf16[256,512]{1,0:T(8,128)(2,1)S(1)}, bf16[256,512]{1,0:T(8,128)(2,1)S(1)}, u32[]{:S(2)}, u32[]{:S(2)}) %collective-permute-start.2) | collective-permute-done | bytes 262176 | tf_op jit(solution)/shard_map/ppermute | solution.py:14
  41.0 0.4 fusion.30
  41.4 0.3 subtract_convert_fusion.4
  41.7 0.1 collective-permute-start.4
  41.8 0.3 fusion.45
  42.1 0.3 fusion.46
  42.4 8.4 %collective-permute-done.4 = bf16[256,512]{1,0:T(8,128)(2,1)S(1)} collective-permute-done((bf16[256,512]{1,0:T(8,128)(2,1)S(1)}, bf16[256,512]{1,0:T(8,128)(2,1)S(1)}, u32[]{:S(2)}, u32[]{:S(2)}) %collective-permute-start.4) | collective-permute-done | bytes 262176 | tf_op jit(solution)/shard_map/ppermute | solution.py:14
  50.8 0.4 fusion.32
  51.2 0.3 fusion.47
  51.5 0.0 collective-permute-done.5
  51.5 1.3 %fusion.33 = bf16[256,512]{1,0:T(8,128)(2,1)S(1)} fusion(bf16[256,512]{1,0:T(8,128)(2,1)S(1)} %collective-permute-done.5, bf16[512,512]{1,0:T(8,128)(2,1)S(1)} %copy-done, bf16[1,4,512,512]{3,2,1,0:T(8,128)(2,1)} %param.7, s32[256]{0:T(256)S(1)} %bitcast.92, s32[512]{0:T(512)S(1)} %copy-done.3), kind=kOutput, calls=%fused_computation.51 | convolution fusion | flops 135266304 | bytes 1313792 | tf_op jit(solution)/shard_map/dot_general | solution.py:19
  52.8 0.3 fusion.48
  53.2 1.3 %fusion.5 = bf16[512,512]{1,0:T(8,128)(2,1)} fusion(f32[512,512]{1,0:T(8,128)S(1)} %fusion.48, f32[512,512]{1,0:T(8,128)S(1)} %fusion.47, f32[512,512]{1,0:T(8,128)S(1)} %fusion.46, f32[512,512]{1,0:T(8,128)S(1)} %fusion.45, f32[512,512]{1,0:T(8,128)S(1)} %fusion.44, f32[512,512]{1,0:T(8,128)S(1)} %convolution_add_fusion.1, ...), kind=kOutput, calls=%fused_computation.7 | convolution fusion | flops 136052736 | bytes 7340032 | tf_op jit(solution)/shard_map/dot_general | solution.py:29
  54.5 0.0 all-gather.3.cloned.1.call-update
  54.5 0.3 subtract_convert_fusion.1
  54.8 0.3 subtract_convert_fusion.2
  55.1 0.8 maximum_bitcast_fusion
  55.9 19.5 %all-gather.3.cloned.1.call-done = bf16[2048,512]{1,0:T(8,128)(2,1)} async-done(((bf16[512,512]{1,0:T(8,128)(2,1)}), bf16[2048,512]{1,0:T(8,128)(2,1)}) %all-gather.3.cloned.1.call-update) | async-done | bytes 2097168 | tf_op jit(solution)/shard_map/all_gather | solution.py:64
  75.4 2.2 %reduce_sum.12 = bf16[512,512]{1,0:T(8,128)(2,1)S(1)} reduce(bf16[4,512,512]{2,1,0:T(8,128)(2,1)} %bitcast.91, bf16[]{:T(256)} %constant.10.clone.1), dimensions={0}, to_apply=%region_0.1 | reduce | flops 786432 | bytes 2621442 | tf_op jit(solution)/shard_map/reduce_sum | solution.py:64
  77.6 1.0 %subtract_convert_fusion = bf16[512,512]{1,0:T(8,128)(2,1)} fusion(bf16[512,512]{1,0:T(8,128)(2,1)S(1)} %reduce_sum.12, bf16[512,512]{1,0:T(8,128)(2,1)S(1)} %copy-done), kind=kLoop, calls=%fused_computation.52 | loop fusion | flops 1310720 | bytes 1572864 | tf_op jit(solution)/shard_map/convert_element_type | solution.py:67
  (3 shorter events, 0.0 us)
Async XLA Ops:
  7.2 2.6 %copy-start = (bf16[512,512]{1,0:T(8,128)(2,1)S(1)}, bf16[512,512]{1,0:T(8,128)(2,1)}, u32[]{:S(2)}) copy-start(bf16[512,512]{1,0:T(8,128)(2,1)} %param.5) | copy-start | bytes 1572868
  7.2 5.9 %copy-start.3 = (s32[512]{0:T(512)S(1)}, s32[512]{0:T(512)}, u32[]{:S(2)}) copy-start(s32[512]{0:T(512)} %param.8) | copy-start | bytes 6148
  7.2 2.6 %copy-start.1 = (bf16[1,512,512]{2,1,0:T(8,128)(2,1)S(1)}, bf16[1,512,512]{2,1,0:T(8,128)(2,1)}, u32[]{:S(2)}) copy-start(bf16[1,512,512]{2,1,0:T(8,128)(2,1)} %param.6) | copy-start | bytes 1572868
  7.2 5.9 %copy-start.2 = (bf16[1,4,512,512]{3,2,1,0:T(8,128)(2,1)S(1)}, bf16[1,4,512,512]{3,2,1,0:T(8,128)(2,1)}, u32[]{:S(2)}) copy-start(bf16[1,4,512,512]{3,2,1,0:T(8,128)(2,1)} %param.7) | copy-start | bytes 6291460
  7.2 68.2 %all-gather.3.cloned.1.call-start = ((), (), s32[]{:S(2)}) async-start(), calls=%async_computation | async-start | bytes 2621440 | tf_op jit(solution)/shard_map/all_gather | solution.py:64
  10.1 13.2 %collective-permute-start.1 = (bf16[256,512]{1,0:T(8,128)(2,1)S(1)}, bf16[256,512]{1,0:T(8,128)(2,1)S(1)}, u32[]{:S(2)}, u32[]{:S(2)}) collective-permute-start(bf16[256,512]{1,0:T(8,128)(2,1)S(1)} %fusion.25), channel_id=1, source_target_pairs={{0,4},{4,8},{8,12},{12,16},{16,20},{20,24},{24,28},{28,0},{1,5},{5... | collective-permute-start | bytes 786440 | tf_op jit(solution)/shard_map/ppermute | solution.py:14
  13.8 14.6 %collective-permute-start = (bf16[256,512]{1,0:T(8,128)(2,1)S(1)}, bf16[256,512]{1,0:T(8,128)(2,1)S(1)}, u32[]{:S(2)}, u32[]{:S(2)}) collective-permute-start(bf16[256,512]{1,0:T(8,128)(2,1)S(1)} %fusion.24), channel_id=1, source_target_pairs={{0,4},{4,8},{8,12},{12,16},{16,20},{20,24},{24,28},{28,0},{1,5},{5... | collective-permute-start | bytes 786440 | tf_op jit(solution)/shard_map/ppermute | solution.py:14
  24.0 10.0 %collective-permute-start.3 = (bf16[256,512]{1,0:T(8,128)(2,1)S(1)}, bf16[256,512]{1,0:T(8,128)(2,1)S(1)}, u32[]{:S(2)}, u32[]{:S(2)}) collective-permute-start(bf16[256,512]{1,0:T(8,128)(2,1)S(1)} %subtract_convert_fusion.5), channel_id=1, source_target_pairs={{0,4},{4,8},{8,12},{12,16},{16,20},{20,24},{24,28},{28,0},{1,5},{5... | collective-permute-start | bytes 786440 | tf_op jit(solution)/shard_map/ppermute | solution.py:14
  29.1 11.9 %collective-permute-start.2 = (bf16[256,512]{1,0:T(8,128)(2,1)S(1)}, bf16[256,512]{1,0:T(8,128)(2,1)S(1)}, u32[]{:S(2)}, u32[]{:S(2)}) collective-permute-start(bf16[256,512]{1,0:T(8,128)(2,1)S(1)} %subtract_convert_fusion.6), channel_id=1, source_target_pairs={{0,4},{4,8},{8,12},{12,16},{16,20},{20,24},{24,28},{28,0},{1,5},{5... | collective-permute-start | bytes 786440 | tf_op jit(solution)/shard_map/ppermute | solution.py:14
  34.7 16.8 %collective-permute-start.5 = (bf16[256,512]{1,0:T(8,128)(2,1)S(1)}, bf16[256,512]{1,0:T(8,128)(2,1)S(1)}, u32[]{:S(2)}, u32[]{:S(2)}) collective-permute-start(bf16[256,512]{1,0:T(8,128)(2,1)S(1)} %subtract_convert_fusion.3), channel_id=1, source_target_pairs={{0,4},{4,8},{8,12},{12,16},{16,20},{20,24},{24,28},{28,0},{1,5},{5... | collective-permute-start | bytes 786440 | tf_op jit(solution)/shard_map/ppermute | solution.py:14
  41.7 9.1 %collective-permute-start.4 = (bf16[256,512]{1,0:T(8,128)(2,1)S(1)}, bf16[256,512]{1,0:T(8,128)(2,1)S(1)}, u32[]{:S(2)}, u32[]{:S(2)}) collective-permute-start(bf16[256,512]{1,0:T(8,128)(2,1)S(1)} %subtract_convert_fusion.4), channel_id=1, source_target_pairs={{0,4},{4,8},{8,12},{12,16},{16,20},{20,24},{24,28},{28,0},{1,5},{5... | collective-permute-start | bytes 786440 | tf_op jit(solution)/shard_map/ppermute | solution.py:14
Sparse Core Ops, SparseCore 0:
  54.6 20.7 all-gather.2
